TPU v7x, 32 devices: a whole 2x2x4 slice. The times are simulated.
32 devices in a mesh: dp: 8 (over z, y), tensor: 4 (over x, core).
Axes of the slice: x: 2, y: 2, z: 4, core: 2. Of those that a mesh axis runs over, the one named last changes fastest.
Arguments:
- tokens: bfloat16 [1024, 16, 768], P(('dp', 'tensor')), may hold values from -6 to 6
- lengths: int32 [16], replicated, may hold values from 1 to 1024, 12288 in all
- dealing: int32 [16], replicated, may hold values from 0 to 15, each once
- project_weight: bfloat16 [768, 2304], P('dp', 'tensor'), may hold values from -0.21875 to 0.21875
- query_projection_bias: float32 [768], replicated, may hold values from -3 to 3
- value_projection_bias: float32 [768], replicated, may hold values from -3 to 3
- attention_output_weight: bfloat16 [768, 768], P('dp', 'tensor'), may hold values from -3.5 to 3.5
- attention_output_bias: float32 [768], replicated, may hold values from -3 to 3
- first_gain: float32 [768], replicated, may hold values from 0.5 to 1.5
- first_shift: float32 [768], replicated, may hold values from -3 to 3
- feed_input_weight: bfloat16 [768, 3072], P('dp', 'tensor'), may hold values from -0.21875 to 0.21875
- feed_input_bias: float32 [3072], replicated, may hold values from -3 to 3
- feed_output_weight: bfloat16 [768, 3072], P('dp', 'tensor'), may hold values from -0.109375 to 0.109375
- feed_output_bias: float32 [768], replicated, may hold values from -3 to 3
- second_gain: float32 [768], replicated, may hold values from 0.5 to 1.5
- second_shift: float32 [768], replicated, may hold values from -3 to 3
- output_grad: bfloat16 [1024, 16, 768], P(('dp', 'tensor')), may hold values from -6 to 6
Outputs:
- layer_output: bfloat16 [1024, 16, 768], P('tensor', 'dp')
- tokens_grad: bfloat16 [1024, 16, 768], P(('dp', 'tensor'))
- project_grad: float32 [768, 2304], P('dp', 'tensor')
- query_bias_grad: float32 [768], P(('dp', 'tensor'))
- value_bias_grad: float32 [768], P(('dp', 'tensor'))
- output_weight_grad: float32 [768, 768], P('dp', 'tensor')
- output_bias_grad: float32 [768], P(('dp', 'tensor'))
- first_gain_grad: float32 [768], P(('dp', 'tensor'))
- first_shift_grad: float32 [768], P(('dp', 'tensor'))
- up_weight_grad: float32 [768, 3072], P('dp', 'tensor')
- up_bias_grad: float32 [3072], P(('dp', 'tensor'))
- down_weight_grad: float32 [768, 3072], P('dp', 'tensor')
- down_bias_grad: float32 [768], P(('dp', 'tensor'))
- second_gain_grad: float32 [768], P(('dp', 'tensor'))
- second_shift_grad: float32 [768], P(('dp', 'tensor'))
Inputs may be any that keep to these rules, and one draw needn't show every extreme that they name: `lengths`: the longest sequence has exactly 1024 tokens. A permutation: sequence s is processed in slot dealing[s], and slot q belongs to data index q // 2.
All inputs are finite; a program needn't handle non-finite values.
Results may differ from a plain program's by a relative error of at most 0.022.
Values may be sent and summed in bfloat16 or wider, within the bound.
A program may use at most 128 MiB of HBM per device.

v0:
```python
from functools import partial
import jax
import jax.numpy as jnp
from jax import lax
from jax.sharding import PartitionSpec as P

HD = 64
EPSILON = 1e-12
MASKED = -1e30


def norm_forward(value, gain, shift):
    centred = value - jnp.mean(value, axis=-1, keepdims=True)
    inverse = lax.rsqrt(jnp.mean(centred * centred, axis=-1, keepdims=True) + EPSILON)
    normed = centred * inverse
    return (normed * gain + shift, normed, inverse)


def norm_backward(upstream, normed, inverse, gain):
    scaled = upstream * gain
    first_mean = jnp.mean(scaled, axis=-1, keepdims=True)
    second_mean = jnp.mean(scaled * normed, axis=-1, keepdims=True)
    return inverse * (scaled - first_mean - normed * second_mean)


def spread_block(values, block_index, length_total):
    blank = jnp.zeros((length_total,), jnp.float32)
    return lax.dynamic_update_slice_in_dim(blank, values, block_index * values.shape[0], 0)


def gather_rows(block):
    return lax.all_gather(block, "tensor", axis=0, tiled=True)


def scatter_rows(partial_sum):
    return lax.psum_scatter(
        partial_sum.astype(jnp.bfloat16), "tensor", scatter_dimension=0, tiled=True
    ).astype(jnp.float32)


def scatter_weight(grad):
    return lax.psum_scatter(
        grad.astype(jnp.bfloat16), "dp", scatter_dimension=0, tiled=True
    ).astype(jnp.float32)


def on_device(
    tokens,
    lengths,
    dealing,
    project_weight,
    query_projection_bias,
    value_projection_bias,
    attention_output_weight,
    attention_output_bias,
    first_gain,
    first_shift,
    feed_input_weight,
    feed_input_bias,
    feed_output_weight,
    feed_output_bias,
    second_gain,
    second_shift,
    output_grad,
):
    n_data = lax.axis_size("dp")
    n_tensor = lax.axis_size("tensor")
    n_all = n_data * n_tensor
    data_index = lax.axis_index("dp")
    tensor_index = lax.axis_index("tensor")
    seq_total = dealing.shape[0]
    seq_here = seq_total // n_data
    piece_rows = tokens.shape[0]
    local_rows = piece_rows * n_data
    seq_rows = local_rows * n_tensor
    width = tokens.shape[2]
    head_cols = attention_output_weight.shape[1]
    heads_here = head_cols // HD
    hidden_cols = feed_input_weight.shape[1]
    score_scale = HD ** (-0.5)
    slot_ids = jnp.arange(seq_total, dtype=jnp.int32)
    placing = (dealing[None, :] == slot_ids[:, None]).astype(jnp.bfloat16)
    send_tokens = jnp.einsum(
        "qs,psd->pqd", placing, tokens, preferred_element_type=jnp.float32
    ).astype(jnp.bfloat16)
    send_grad = jnp.einsum(
        "qs,psd->pqd", placing, output_grad, preferred_element_type=jnp.float32
    ).astype(jnp.bfloat16)
    tokens_here = lax.all_to_all(send_tokens, "dp", split_axis=1, concat_axis=0, tiled=True)
    cotangent_here = lax.all_to_all(send_grad, "dp", split_axis=1, concat_axis=0, tiled=True)
    my_slots = data_index * seq_here + jnp.arange(seq_here, dtype=jnp.int32)
    mine = dealing[None, :] == my_slots[:, None]
    seq_length = jnp.sum(jnp.where(mine, lengths[None, :], 0), axis=1)
    row_ids = jnp.arange(seq_rows, dtype=jnp.int32)
    owner_rows = row_ids // local_rows
    inner_rows = row_ids % local_rows
    position = (
        inner_rows // piece_rows * n_tensor + owner_rows
    ) * piece_rows + inner_rows % piece_rows
    key_valid = position[None, :] < seq_length[:, None]
    project_full = lax.all_gather(project_weight, "dp", axis=0, tiled=True)
    output_full = lax.all_gather(attention_output_weight, "dp", axis=0, tiled=True)
    up_full = lax.all_gather(feed_input_weight, "dp", axis=0, tiled=True)
    down_full = lax.all_gather(feed_output_weight, "dp", axis=0, tiled=True)
    query_part = lax.dynamic_slice_in_dim(
        query_projection_bias, tensor_index * head_cols, head_cols
    )
    value_part = lax.dynamic_slice_in_dim(
        value_projection_bias, tensor_index * head_cols, head_cols
    )
    project_bias = jnp.concatenate([query_part, jnp.zeros_like(query_part), value_part])
    up_bias_here = lax.dynamic_slice_in_dim(
        feed_input_bias, tensor_index * hidden_cols, hidden_cols
    )

    def split_heads(qkv_block):
        query_rows = qkv_block[:, :head_cols].reshape(seq_rows, heads_here, HD)
        key_rows = qkv_block[:, head_cols : 2 * head_cols].reshape(seq_rows, heads_here, HD)
        value_rows = qkv_block[:, 2 * head_cols :].reshape(seq_rows, heads_here, HD)
        return (query_rows, key_rows, value_rows)

    def masked_scores(query_rows, key_rows, valid_keys):
        raw_scores = (
            jnp.einsum("qhe,khe->hqk", query_rows, key_rows, preferred_element_type=jnp.float32)
            * score_scale
        )
        return jnp.where(valid_keys[None, None, :], raw_scores, MASKED)

    def attend(qkv_block, valid_keys):
        query_rows, key_rows, value_rows = split_heads(qkv_block)
        scores = masked_scores(query_rows, key_rows, valid_keys)
        row_max = jnp.max(scores, axis=-1, keepdims=True)
        exponent = jnp.exp(scores - row_max)
        row_total = jnp.sum(exponent, axis=-1, keepdims=True)
        weights = (exponent / row_total).astype(jnp.bfloat16)
        mixed_heads = jnp.einsum(
            "hqk,khe->qhe", weights, value_rows, preferred_element_type=jnp.float32
        )
        return (
            mixed_heads.reshape(seq_rows, head_cols).astype(jnp.bfloat16),
            (row_max + jnp.log(row_total))[..., 0],
        )

    def attend_back(qkv_block, valid_keys, row_lse, grad_block):
        query_rows, key_rows, value_rows = split_heads(qkv_block)
        weights = jnp.exp(masked_scores(query_rows, key_rows, valid_keys) - row_lse[..., None])
        grad_heads = grad_block.reshape(seq_rows, heads_here, HD)
        grad_weights = jnp.einsum(
            "qhe,khe->hqk", grad_heads, value_rows, preferred_element_type=jnp.float32
        )
        inner_sum = jnp.sum(weights * grad_weights, axis=-1, keepdims=True)
        grad_scores = (weights * (grad_weights - inner_sum)).astype(jnp.bfloat16)
        grad_query = (
            jnp.einsum("hqk,khe->qhe", grad_scores, key_rows, preferred_element_type=jnp.float32)
            * score_scale
        )
        grad_key = (
            jnp.einsum("hqk,qhe->khe", grad_scores, query_rows, preferred_element_type=jnp.float32)
            * score_scale
        )
        grad_value = jnp.einsum(
            "hqk,qhe->khe",
            weights.astype(jnp.bfloat16),
            grad_heads,
            preferred_element_type=jnp.float32,
        )
        joined = jnp.concatenate(
            [
                grad_query.reshape(seq_rows, head_cols),
                grad_key.reshape(seq_rows, head_cols),
                grad_value.reshape(seq_rows, head_cols),
            ],
            axis=-1,
        )
        return joined.astype(jnp.bfloat16)

    gelu_exact = partial(jax.nn.gelu, approximate=False)
    seqs = range(seq_here)
    inputs_full = [gather_rows(tokens_here[:, s, :]) for s in seqs]
    projected = [
        (
            jnp.dot(inputs_full[s], project_full, preferred_element_type=jnp.float32) + project_bias
        ).astype(jnp.bfloat16)
        for s in seqs
    ]
    attended = [attend(projected[s], key_valid[s]) for s in seqs]
    mixed = [a[0] for a in attended]
    log_total = [a[1] for a in attended]
    branch = [
        scatter_rows(
            lax.dot_general(
                mixed[s], output_full, (((1,), (1,)), ((), ())), preferred_element_type=jnp.float32
            )
        )
        for s in seqs
    ]
    first = [
        norm_forward(
            tokens_here[:, s, :].astype(jnp.float32) + branch[s] + attention_output_bias,
            first_gain,
            first_shift,
        )
        for s in seqs
    ]
    first_full = [gather_rows(first[s][0].astype(jnp.bfloat16)) for s in seqs]
    preact = [
        jnp.dot(first_full[s], up_full, preferred_element_type=jnp.float32) + up_bias_here
        for s in seqs
    ]
    gelu_pairs = [jax.vjp(gelu_exact, preact[s]) for s in seqs]
    hidden = [g[0].astype(jnp.bfloat16) for g in gelu_pairs]
    feed = [
        scatter_rows(
            lax.dot_general(
                hidden[s], down_full, (((1,), (1,)), ((), ())), preferred_element_type=jnp.float32
            )
        )
        for s in seqs
    ]
    second = [
        norm_forward(first[s][0] + feed[s] + feed_output_bias, second_gain, second_shift)
        for s in seqs
    ]
    layer_output = jnp.stack([second[s][0] for s in seqs], axis=1).astype(jnp.bfloat16)
    cot = [cotangent_here[:, s, :].astype(jnp.float32) for s in seqs]
    second_gain_part = sum((jnp.sum(cot[s] * second[s][1], axis=0) for s in seqs))
    second_shift_part = sum((jnp.sum(cot[s], axis=0) for s in seqs))
    grad_second = [norm_backward(cot[s], second[s][1], second[s][2], second_gain) for s in seqs]
    down_bias_part = sum((jnp.sum(grad_second[s], axis=0) for s in seqs))
    grad_feed_full = [gather_rows(grad_second[s].astype(jnp.bfloat16)) for s in seqs]
    grad_hidden = [
        jnp.dot(grad_feed_full[s], down_full, preferred_element_type=jnp.float32) for s in seqs
    ]
    down_grad = sum(
        (
            lax.dot_general(
                grad_feed_full[s],
                hidden[s],
                (((0,), (0,)), ((), ())),
                preferred_element_type=jnp.float32,
            )
            for s in seqs
        )
    )
    down_shard = scatter_weight(down_grad)
    grad_preact = [gelu_pairs[s][1](grad_hidden[s])[0].astype(jnp.bfloat16) for s in seqs]
    up_grad = sum(
        (
            lax.dot_general(
                first_full[s],
                grad_preact[s],
                (((0,), (0,)), ((), ())),
                preferred_element_type=jnp.float32,
            )
            for s in seqs
        )
    )
    up_shard = scatter_weight(up_grad)
    up_bias_part = sum((jnp.sum(grad_preact[s], axis=0, dtype=jnp.float32) for s in seqs))
    grad_first = [
        grad_second[s]
        + scatter_rows(
            lax.dot_general(
                grad_preact[s],
                up_full,
                (((1,), (1,)), ((), ())),
                preferred_element_type=jnp.float32,
            )
        )
        for s in seqs
    ]
    first_gain_part = sum((jnp.sum(grad_first[s] * first[s][1], axis=0) for s in seqs))
    first_shift_part = sum((jnp.sum(grad_first[s], axis=0) for s in seqs))
    grad_residual = [
        norm_backward(grad_first[s], first[s][1], first[s][2], first_gain) for s in seqs
    ]
    output_bias_part = sum((jnp.sum(grad_residual[s], axis=0) for s in seqs))
    early_vectors = jnp.concatenate(
        [
            v.reshape(n_all, -1)
            for v in (
                output_bias_part,
                first_gain_part,
                first_shift_part,
                spread_block(up_bias_part, tensor_index, hidden_cols * n_tensor),
                down_bias_part,
                second_gain_part,
                second_shift_part,
            )
        ],
        axis=1,
    )
    early_reduced = lax.psum_scatter(
        early_vectors, ("dp", "tensor"), scatter_dimension=0, tiled=True
    )[0]
    branch_grad_full = [gather_rows(grad_residual[s].astype(jnp.bfloat16)) for s in seqs]
    grad_mixed = [
        jnp.dot(branch_grad_full[s], output_full, preferred_element_type=jnp.float32).astype(
            jnp.bfloat16
        )
        for s in seqs
    ]
    output_grad_weight = sum(
        (
            lax.dot_general(
                branch_grad_full[s],
                mixed[s],
                (((0,), (0,)), ((), ())),
                preferred_element_type=jnp.float32,
            )
            for s in seqs
        )
    )
    output_shard = scatter_weight(output_grad_weight)
    grad_projected = [
        attend_back(projected[s], key_valid[s], log_total[s], grad_mixed[s]) for s in seqs
    ]
    project_grad = sum(
        (
            lax.dot_general(
                inputs_full[s],
                grad_projected[s],
                (((0,), (0,)), ((), ())),
                preferred_element_type=jnp.float32,
            )
            for s in seqs
        )
    )
    project_shard = scatter_weight(project_grad)
    bias_sums = sum((jnp.sum(grad_projected[s], axis=0, dtype=jnp.float32) for s in seqs))
    late_vectors = jnp.concatenate(
        [
            spread_block(bias_sums[:head_cols], tensor_index, width).reshape(n_all, -1),
            spread_block(bias_sums[2 * head_cols :], tensor_index, width).reshape(n_all, -1),
        ],
        axis=1,
    )
    late_reduced = lax.psum_scatter(
        late_vectors, ("dp", "tensor"), scatter_dimension=0, tiled=True
    )[0]
    grad_inputs = [
        grad_residual[s]
        + scatter_rows(
            lax.dot_general(
                grad_projected[s],
                project_full,
                (((1,), (1,)), ((), ())),
                preferred_element_type=jnp.float32,
            )
        )
        for s in seqs
    ]
    grad_here = jnp.stack(grad_inputs, axis=1).astype(jnp.bfloat16)
    returned = lax.all_to_all(grad_here, "dp", split_axis=0, concat_axis=1, tiled=True)
    tokens_grad = jnp.einsum(
        "qs,pqd->psd", placing, returned, preferred_element_type=jnp.float32
    ).astype(jnp.bfloat16)
    vec_block = width // n_all
    early_split = [vec_block] * 3 + [hidden_cols * n_tensor // n_all] + [vec_block] * 3
    offsets = [sum(early_split[:k]) for k in range(len(early_split) + 1)]
    early = [early_reduced[offsets[k] : offsets[k + 1]] for k in range(len(early_split))]
    late = [late_reduced[:vec_block], late_reduced[vec_block:]]
    return (
        layer_output,
        tokens_grad,
        project_shard,
        late[0],
        late[1],
        output_shard,
        early[0],
        early[1],
        early[2],
        up_shard,
        early[3],
        down_shard,
        early[4],
        early[5],
        early[6],
    )


def solution(mesh):
    in_specs = (
        P(("dp", "tensor"), None, None),
        P(),
        P(),
        P("dp", "tensor"),
        P(),
        P(),
        P("dp", "tensor"),
        P(),
        P(),
        P(),
        P("dp", "tensor"),
        P(),
        P("dp", "tensor"),
        P(),
        P(),
        P(),
        P(("dp", "tensor"), None, None),
    )
    out_specs = (
        P("tensor", "dp", None),
        P(("dp", "tensor"), None, None),
        P("dp", "tensor"),
        P(("dp", "tensor")),
        P(("dp", "tensor")),
        P("dp", "tensor"),
        P(("dp", "tensor")),
        P(("dp", "tensor")),
        P(("dp", "tensor")),
        P("dp", "tensor"),
        P(("dp", "tensor")),
        P("dp", "tensor"),
        P(("dp", "tensor")),
        P(("dp", "tensor")),
        P(("dp", "tensor")),
    )
    return jax.shard_map(
        on_device, mesh=mesh, in_specs=in_specs, out_specs=out_specs, check_vma=False
    )
```

profile of v0, /device:TPU:0, one launch (start us, length us, event | category | flops | bytes accessed | tf_op | source)
XLA Modules:
  0.0 850.2 jit_solution(14724456239618128440)
XLA Ops:
  10.6 27.4 %all_to_all.54 = bf16[32,16,768]{2,0,1:T(8,128)(2,1)S(1)} all-to-all(bf16[32,16,768]{2,0,1:T(8,128)(2,1)S(1)} %copy.78), channel_id=1, replica_groups=mesh['dp'=8,'tensor'=4] {'dp'}, dimensions={1} | all-to-all | bytes 1572864 | tf_op jit(solution)/shard_map/all_to_all | solution.py:89
  41.7 31.2 %all_gather.38 = bf16[768,192]{1,0:T(8,128)(2,1)S(1)} all-gather(bf16[96,192]{1,0:T(8,128)(2,1)S(1)} %copy-done.49), channel_id=1, replica_groups=mesh['dp'=8,'tensor'=4] {'dp'}, dimensions={0}, use_global_device_ids=true | all-gather | bytes 331776 | tf_op jit(solution)/shard_map/all_gather | solution.py:102
  72.9 32.5 %all_gather.37 = bf16[768,576]{1,0:T(8,128)(2,1)S(1)} all-gather(bf16[96,576]{1,0:T(8,128)(2,1)S(1)} %copy-done.45), channel_id=1, replica_groups=mesh['dp'=8,'tensor'=4] {'dp'}, dimensions={0}, use_global_device_ids=true | all-gather | bytes 995328 | tf_op jit(solution)/shard_map/all_gather | solution.py:101
  106.4 2.5 add_convert_fusion.4
  109.1 3.2 add_convert_fusion.5
  112.4 2.4 fusion.117
  116.6 2.8 copy-done.2
  119.5 2.3 fusion.47
  124.3 2.3 fusion.118
  128.4 3.1 copy-done.3
  131.5 2.3 fusion.46
  136.4 14.9 %reduce-scatter.13.cloned.1.call-done = bf16[256,768]{1,0:T(8,128)(2,1)} async-done(((bf16[1024,768]{1,0:T(8,128)(2,1)}), bf16[256,768]{1,0:T(8,128)(2,1)}) %reduce-scatter.13.cloned.1.call-update) | async-done | bytes 393232 | tf_op jit(solution)/shard_map/reduce_scatter | solution.py:36
  152.6 29.1 %reduce-scatter.17.cloned.1.call-done = bf16[256,768]{1,0:T(8,128)(2,1)} async-done(((bf16[1024,768]{1,0:T(8,128)(2,1)}), bf16[256,768]{1,0:T(8,128)(2,1)}) %reduce-scatter.17.cloned.1.call-update) | async-done | bytes 393232 | tf_op jit(solution)/shard_map/reduce_scatter | solution.py:36
  184.5 2.3 fusion.68
  189.2 17.3 %all-gather.19.cloned.1.call-done = bf16[1024,768]{1,0:T(8,128)(2,1)} async-done(((bf16[256,768]{1,0:T(8,128)(2,1)}), bf16[1024,768]{1,0:T(8,128)(2,1)}) %all-gather.19.cloned.1.call-update) | async-done | bytes 1572880 | tf_op jit(solution)/shard_map/all_gather | solution.py:32
  206.5 4.9 fusion.119
  211.4 16.7 %all-gather.13.cloned.1.call-done = bf16[1024,768]{1,0:T(8,128)(2,1)} async-done(((bf16[256,768]{1,0:T(8,128)(2,1)}), bf16[1024,768]{1,0:T(8,128)(2,1)}) %all-gather.13.cloned.1.call-update) | async-done | bytes 1572880 | tf_op jit(solution)/shard_map/all_gather | solution.py:32
  228.1 17.3 %multiply_convert_fusion.3 = (bf16[1024,768]{1,0:T(8,128)(2,1)}, f32[1024,768]{1,0:T(8,128)}, bf16[1024,768]{1,0:T(8,128)(2,1)}, f32[1024,768]{1,0:T(8,128)}, f32[1024,768]{1,0:T(8,128)}) fusion(f32[768]{0:T(1024)S(1)} %dynamic_slice.11, f32[1024,768]{1,0:T(8,128)} %fusion.119, bf16[1024,768]{1,0:T(8,128)(2,1)} %all-gather.13.cloned.1.call-done, ...), kind=kOutput, calls=%fused_computation.43 | convolution fusion | flops 1311768576 | bytes 18484224 | tf_op jit(solution)/shard_map/dot_general | solution.py:207
  245.4 26.3 %all-gather.17.cloned.1.call-done = bf16[768,768]{1,0:T(8,128)(2,1)} async-done(((bf16[96,768]{1,0:T(8,128)(2,1)}), bf16[768,768]{1,0:T(8,128)(2,1)}) %all-gather.17.cloned.1.call-update) | async-done | bytes 1179664 | tf_op jit(solution)/shard_map/all_gather | solution.py:104
  271.7 4.3 convolution_convert_fusion.6
  276.1 4.4 convolution_convert_fusion.4
  282.0 21.2 %all_to_all.55 = bf16[32,16,768]{2,0,1:T(8,128)(2,1)S(1)} all-to-all(bf16[32,16,768]{2,0,1:T(8,128)(2,1)S(1)} %copy.83), channel_id=1, replica_groups=mesh['dp'=8,'tensor'=4] {'dp'}, dimensions={1} | all-to-all | bytes 1572864 | tf_op jit(solution)/shard_map/all_to_all | solution.py:90
  303.4 29.6 %reduce-scatter.19.cloned.1.call-done = bf16[256,768]{1,0:T(8,128)(2,1)} async-done(((bf16[1024,768]{1,0:T(8,128)(2,1)}), bf16[256,768]{1,0:T(8,128)(2,1)}) %reduce-scatter.19.cloned.1.call-update) | async-done | bytes 393232 | tf_op jit(solution)/shard_map/reduce_scatter | solution.py:36
  333.0 1.9 fusion.110
  336.7 3.2 fusion.108
  341.0 18.6 %all-gather.21.cloned.1.call-done = bf16[1024,768]{1,0:T(8,128)(2,1)} async-done(((bf16[256,768]{1,0:T(8,128)(2,1)}), bf16[1024,768]{1,0:T(8,128)(2,1)}) %all-gather.21.cloned.1.call-update) | async-done | bytes 1572880 | tf_op jit(solution)/shard_map/all_gather | solution.py:32
  359.7 4.8 fusion.120
  364.4 16.3 %all-gather.25.cloned.1.call-done = bf16[1024,768]{1,0:T(8,128)(2,1)} async-done(((bf16[256,768]{1,0:T(8,128)(2,1)}), bf16[1024,768]{1,0:T(8,128)(2,1)}) %all-gather.25.cloned.1.call-update) | async-done | bytes 1572880 | tf_op jit(solution)/shard_map/all_gather | solution.py:32
  380.8 11.5 %convert_reduce_fusion = (f32[768]{0:T(1024)}, bf16[1024,768]{1,0:T(8,128)(2,1)}, f32[768]{0:T(1024)}, bf16[1024,768]{1,0:T(8,128)(2,1)S(1)}) fusion(f32[1024,768]{1,0:T(8,128)} %get-tuple-element.152, f32[1024,768]{1,0:T(8,128)} %fusion.119, f32[768]{0:T(1024)} %copy-done.58, f32[1024,768]{1,0:T(8,128)} %fusion.120, f32[1024,768]{1,0:T(8,128)} %get-tuple-element.119, ...), kind=kOutput, calls=%fused_computation.26 | convolution fusion | flops 1234696704 | bytes 21636096 | tf_op jit(solution)/shard_map/dot_general | solution.py:232
  393.5 2.6 convolution_convert_fusion.3
  396.1 4.4 convolution_convert_fusion.2
  400.6 23.6 %reduce-scatter.21.cloned.1.call-done = bf16[256,768]{1,0:T(8,128)(2,1)} async-done(((bf16[1024,768]{1,0:T(8,128)(2,1)}), bf16[256,768]{1,0:T(8,128)(2,1)}) %reduce-scatter.21.cloned.1.call-update) | async-done | bytes 393232 | tf_op jit(solution)/shard_map/reduce_scatter | solution.py:36
  424.1 30.4 %reduce-scatter.25.cloned.1.call-done = bf16[256,768]{1,0:T(8,128)(2,1)} async-done(((bf16[1024,768]{1,0:T(8,128)(2,1)}), bf16[256,768]{1,0:T(8,128)(2,1)}) %reduce-scatter.25.cloned.1.call-update) | async-done | bytes 393232 | tf_op jit(solution)/shard_map/reduce_scatter | solution.py:36
  454.5 3.1 multiply_reduce_fusion.3
  457.7 2.9 fusion.107
  463.9 1.9 convert_element_type.237
  466.3 15.8 %all-gather.27.cloned.1.call-done = bf16[1024,768]{1,0:T(8,128)(2,1)} async-done(((bf16[256,768]{1,0:T(8,128)(2,1)}), bf16[1024,768]{1,0:T(8,128)(2,1)}) %all-gather.27.cloned.1.call-update) | async-done | bytes 1572880 | tf_op jit(solution)/shard_map/all_gather | solution.py:32
  482.1 2.1 convolution_convert_fusion.11
  484.3 6.1 multiply_reduce_fusion
  493.0 5.2 multiply_convert_fusion
  498.3 5.0 fusion.38
  504.5 2.0 fusion.42
  506.6 2.6 convolution_convert_fusion
  509.5 2.1 convolution_convert_fusion.12
  511.7 6.4 multiply_reduce_fusion.1
  520.7 5.2 multiply_convert_fusion.1
  525.9 5.0 fusion.36
  532.2 2.0 fusion.39
  534.3 2.6 convolution_convert_fusion.1
  537.0 3.5 fusion.123
  540.5 2.6 add_convert_fusion.2
  543.4 3.7 fusion.122
  547.2 2.6 add_convert_fusion.3
  553.6 2.1 fusion.121
  557.2 3.2 fusion.24
  560.4 2.4 add_convert_fusion.6
  562.9 1.9 fusion.75
  564.8 3.1 reduce-scatter.23.cloned.1.call-done
  571.8 5.5 all-to-all-start.2
  578.2 62.9 %reduce-scatter.35.cloned.1.call-done = bf16[96,768]{1,0:T(8,128)(2,1)} async-done(((bf16[768,768]{1,0:T(8,128)(2,1)}), bf16[96,768]{1,0:T(8,128)(2,1)}) %reduce-scatter.35.cloned.1.call-update) | async-done | bytes 147472 | tf_op jit(solution)/shard_map/reduce_scatter | solution.py:42
  642.7 65.5 %reduce-scatter.33.cloned.1.call-done = bf16[96,768]{1,0:T(8,128)(2,1)} async-done(((bf16[768,768]{1,0:T(8,128)(2,1)}), bf16[96,768]{1,0:T(8,128)(2,1)}) %reduce-scatter.33.cloned.1.call-update) | async-done | bytes 147472 | tf_op jit(solution)/shard_map/reduce_scatter | solution.py:42
  716.4 40.2 %all-reduce.2 = (f32[32,48]{1,0:T(8,128)S(1)}, f32[32,240]{1,0:T(8,128)S(1)}) all-reduce(f32[32,48]{1,0:T(8,128)S(1)} %pad_maximum_fusion.4, f32[32,240]{1,0:T(8,128)} %concatenate.21), channel_id=13, replica_groups=mesh['dp'=8,'tensor'=4] {'dp','tensor'}, use_global_device_ids=true, to_apply=%region_34.35.clone | all-reduce | flops 9216 | bytes 73728
  758.5 14.3 %reduce-scatter.31.cloned.1.call-done = bf16[96,192]{1,0:T(8,128)(2,1)} async-done(((bf16[768,192]{1,0:T(8,128)(2,1)}), bf16[96,192]{1,0:T(8,128)(2,1)}) %reduce-scatter.31.cloned.1.call-update) | async-done | bytes 36880 | tf_op jit(solution)/shard_map/reduce_scatter | solution.py:42
  774.2 64.8 %reduce-scatter.29.cloned.1.call-done = bf16[96,576]{1,0:T(8,128)(2,1)} async-done(((bf16[768,576]{1,0:T(8,128)(2,1)}), bf16[96,576]{1,0:T(8,128)(2,1)}) %reduce-scatter.29.cloned.1.call-update) | async-done | bytes 110608 | tf_op jit(solution)/shard_map/reduce_scatter | solution.py:42
  (293 shorter events, 67.1 us)
Async XLA Ops:
  8.0 97.4 %all-gather.31.cloned.1.call-start = ((), (), s32[]{:S(2)}) async-start(), calls=%async_computation.36 | async-start | bytes 1966080 | tf_op jit(solution)/shard_map/all_gather | solution.py:32
  10.5 30.9 %copy-start.56 = (s32[16]{0:T(128)S(1)}, s32[16]{0:T(128)}, u32[]{:S(2)}) copy-start(s32[16]{0:T(128)} %param.19) | copy-start | bytes 196
  10.5 30.9 %copy-start.59 = (s32[16]{0:T(128)S(1)}, s32[16]{0:T(128)}, u32[]{:S(2)}) copy-start(s32[16]{0:T(128)} %param.18) | copy-start | bytes 196
  10.6 31.2 %copy-start.49 = (bf16[96,192]{1,0:T(8,128)(2,1)S(1)}, bf16[96,192]{1,0:T(8,128)(2,1)}, u32[]{:S(2)}) copy-start(bf16[96,192]{1,0:T(8,128)(2,1)} %param.23) | copy-start | bytes 110596
  10.6 62.3 %copy-start.45 = (bf16[96,576]{1,0:T(8,128)(2,1)S(1)}, bf16[96,576]{1,0:T(8,128)(2,1)}, u32[]{:S(2)}) copy-start(bf16[96,576]{1,0:T(8,128)(2,1)} %param.20) | copy-start | bytes 331780
  39.0 70.1 %all-gather.29.cloned.1.call-start = ((), (), s32[]{:S(2)}) async-start(), calls=%async_computation.35 | async-start | bytes 1966080 | tf_op jit(solution)/shard_map/all_gather | solution.py:32
  39.7 111.6 %reduce-scatter.13.cloned.1.call-start = ((), (), s32[]{:S(2)}) async-start(), calls=%async_computation.15 | async-start | bytes 1966080 | tf_op jit(solution)/shard_map/reduce_scatter | solution.py:36
  109.0 15.2 %copy-start.17 = (bf16[1024,192]{0,1:T(8,128)(2,1)}, bf16[1024,192]{0,1:T(8,128)(2,1)S(1)}, u32[]{:S(2)}) copy-start(bf16[1024,192]{0,1:T(8,128)(2,1)S(1)} %get-tuple-element.127) | copy-start | bytes 1179652
  109.0 15.2 %copy-start.19 = (bf16[1024,192]{0,1:T(8,128)(2,1)}, bf16[1024,192]{0,1:T(8,128)(2,1)S(1)}, u32[]{:S(2)}) copy-start(bf16[1024,192]{0,1:T(8,128)(2,1)S(1)} %get-tuple-element.128) | copy-start | bytes 1179652
  109.0 19.4 %copy-start.23 = (bf16[1024,192]{0,1:T(8,128)(2,1)}, bf16[1024,192]{0,1:T(8,128)(2,1)S(1)}, u32[]{:S(2)}) copy-start(bf16[1024,192]{0,1:T(8,128)(2,1)S(1)} %get-tuple-element.129) | copy-start | bytes 1179652
  116.5 5.3 copy-start.46
  123.7 58.0 %reduce-scatter.17.cloned.1.call-start = ((), (), s32[]{:S(2)}) async-start(), calls=%async_computation.20 | async-start | bytes 1966080 | tf_op jit(solution)/shard_map/reduce_scatter | solution.py:36
  128.4 5.5 copy-start.47
  133.9 49.3 %copy-start.25 = (bf16[3,64,1024]{2,1,0:T(8,128)(2,1)}, bf16[3,64,1024]{2,1,0:T(8,128)(2,1)S(1)}, u32[]{:S(2)}) copy-start(bf16[3,64,1024]{2,1,0:T(8,128)(2,1)S(1)} %fusion.46) | copy-start | bytes 1179652
  133.9 17.4 %copy-start.42 = (f32[768]{0:T(1024)S(1)}, f32[768]{0:T(1024)}, u32[]{:S(2)}) copy-start(f32[768]{0:T(1024)} %param.24) | copy-start | bytes 9220
  133.9 50.6 %copy-start.48 = (f32[768]{0:T(1024)S(1)}, f32[768]{0:T(1024)}, u32[]{:S(2)}) copy-start(f32[768]{0:T(1024)} %param.25) | copy-start | bytes 9220
  133.9 50.6 %copy-start.54 = (f32[768]{0:T(1024)S(1)}, f32[768]{0:T(1024)}, u32[]{:S(2)}) copy-start(f32[768]{0:T(1024)} %param.26) | copy-start | bytes 9220
  135.7 53.5 %all-gather.15.cloned.1.call-start = ((), (), s32[]{:S(2)}) async-start(), calls=%async_computation.17 | async-start | bytes 1327104 | tf_op jit(solution)/shard_map/all_gather | solution.py:103
  136.3 70.2 %all-gather.19.cloned.1.call-start = ((), (), s32[]{:S(2)}) async-start(), calls=%async_computation.21 | async-start | bytes 1966080 | tf_op jit(solution)/shard_map/all_gather | solution.py:32
  151.3 33.2 %copy-start.6 = (bf16[256,768]{1,0:T(8,128)(2,1)S(1)}, bf16[256,768]{1,0:T(8,128)(2,1)}, u32[]{:S(2)}) copy-start(bf16[256,768]{1,0:T(8,128)(2,1)} %reduce-scatter.13.cloned.1.call-done) | copy-start | bytes 1179652
  183.2 28.1 %copy-start.51 = (f32[256]{0:T(256)}, f32[256]{0:T(256)S(1)}, u32[]{:S(2)}) copy-start(f32[256]{0:T(256)S(1)} %get-tuple-element.164) | copy-start | bytes 3076
  184.5 26.9 %copy-start.50 = (f32[256]{0:T(256)}, f32[256]{0:T(256)S(1)}, u32[]{:S(2)}) copy-start(f32[256]{0:T(256)S(1)} %add_rsqrt_fusion.1) | copy-start | bytes 3076
  186.9 41.2 %all-gather.13.cloned.1.call-start = ((), (), s32[]{:S(2)}) async-start(), calls=%async_computation.16 | async-start | bytes 1966080 | tf_op jit(solution)/shard_map/all_gather | solution.py:32
  187.5 84.2 %all-gather.17.cloned.1.call-start = ((), (), s32[]{:S(2)}) async-start(), calls=%async_computation.18 | async-start | bytes 1327104 | tf_op jit(solution)/shard_map/all_gather | solution.py:104
  188.2 115.2 %reduce-scatter.15.cloned.1.call-start = ((), (), s32[]{:S(2)}) async-start(), calls=%async_computation.19 | async-start | bytes 1966080 | tf_op jit(solution)/shard_map/reduce_scatter | solution.py:36
  189.2 38.8 %copy-start.58 = (f32[768]{0:T(1024)}, f32[768]{0:T(1024)S(1)}, u32[]{:S(2)}) copy-start(f32[768]{0:T(1024)S(1)} %dynamic_slice.11) | copy-start | bytes 9220
  189.2 38.8 %copy-start.63 = (bf16[768,768]{1,0:T(8,128)(2,1)S(1)}, bf16[768,768]{1,0:T(8,128)(2,1)}, u32[]{:S(2)}) copy-start(bf16[768,768]{1,0:T(8,128)(2,1)} %all-gather.15.cloned.1.call-done) | copy-start | bytes 3538948
  276.0 57.0 %reduce-scatter.19.cloned.1.call-start = ((), (), s32[]{:S(2)}) async-start(), calls=%async_computation.22 | async-start | bytes 1966080 | tf_op jit(solution)/shard_map/reduce_scatter | solution.py:36
  280.5 52.5 %copy-start.7 = (bf16[256,768]{1,0:T(8,128)(2,1)S(1)}, bf16[256,768]{1,0:T(8,128)(2,1)}, u32[]{:S(2)}) copy-start(bf16[256,768]{1,0:T(8,128)(2,1)} %reduce-scatter.17.cloned.1.call-done) | copy-start | bytes 1179652
  280.5 79.1 %all-gather.21.cloned.1.call-start = ((), (), s32[]{:S(2)}) async-start(), calls=%async_computation.23 | async-start | bytes 1966080 | tf_op jit(solution)/shard_map/all_gather | solution.py:32
  303.3 32.1 %copy-start.55 = (f32[768]{0:T(1024)S(1)}, f32[768]{0:T(1024)}, u32[]{:S(2)}) copy-start(f32[768]{0:T(1024)} %param.31) | copy-start | bytes 9220
  339.9 40.9 %all-gather.25.cloned.1.call-start = ((), (), s32[]{:S(2)}) async-start(), calls=%async_computation.27 | async-start | bytes 1966080 | tf_op jit(solution)/shard_map/all_gather | solution.py:32
  340.8 83.4 %reduce-scatter.21.cloned.1.call-start = ((), (), s32[]{:S(2)}) async-start(), calls=%async_computation.24 | async-start | bytes 1966080 | tf_op jit(solution)/shard_map/reduce_scatter | solution.py:36
  380.8 12.7 %copy-start.64 = (bf16[768,768]{1,0:T(8,128)(2,1)S(1)}, bf16[768,768]{1,0:T(8,128)(2,1)}, u32[]{:S(2)}) copy-start(bf16[768,768]{1,0:T(8,128)(2,1)} %all-gather.15.cloned.1.call-done) | copy-start | bytes 3538948
  396.1 58.5 %reduce-scatter.25.cloned.1.call-start = ((), (), s32[]{:S(2)}) async-start(), calls=%async_computation.28 | async-start | bytes 1966080 | tf_op jit(solution)/shard_map/reduce_scatter | solution.py:36
  400.5 81.6 %all-gather.27.cloned.1.call-start = ((), (), s32[]{:S(2)}) async-start(), calls=%async_computation.29 | async-start | bytes 1966080 | tf_op jit(solution)/shard_map/all_gather | solution.py:32
  460.6 23.6 %copy-start.24 = (bf16[1024,192]{0,1:T(8,128)(2,1)S(1)}, bf16[1024,192]{0,1:T(8,128)(2,1)}, u32[]{:S(2)}) copy-start(bf16[1024,192]{0,1:T(8,128)(2,1)} %copy-done.23) | copy-start | bytes 1179652
  462.4 47.2 %all-gather.23.cloned.1.call-start = ((), (), s32[]{:S(2)}) async-start(), calls=%async_computation.25 | async-start | bytes 1966080 | tf_op jit(solution)/shard_map/all_gather | solution.py:32
  465.8 97.0 %reduce-scatter.27.cloned.1.call-start = ((), (), s32[]{:S(2)}) async-start(), calls=%async_computation.30 | async-start | bytes 1966080 | tf_op jit(solution)/shard_map/reduce_scatter | solution.py:36
  484.2 6.1 slice-start.3
  484.2 7.3 slice-start.4
  484.3 8.8 %slice-start.5 = ((s8[12582912]{0:T(1024)(128)(4,1)}), s8[4194304]{0:T(1024)(128)(4,1)S(1)}, s32[]{:S(2)}) async-start(s8[12582912]{0:T(1024)(128)(4,1)} %bitcast.236), calls=%async_computation.42 | async-start | bytes 8388608
  493.0 5.2 copy-start.20
  498.3 5.0 copy-start.4
  498.3 5.0 copy-start.18
  509.3 58.6 %reduce-scatter.23.cloned.1.call-start = ((), (), s32[]{:S(2)}) async-start(), calls=%async_computation.26 | async-start | bytes 1966080 | tf_op jit(solution)/shard_map/reduce_scatter | solution.py:36
  511.6 6.5 slice-start
  511.6 7.9 slice-start.1
  511.7 9.1 %slice-start.2 = ((s8[12582912]{0:T(1024)(128)(4,1)}), s8[4194304]{0:T(1024)(128)(4,1)S(1)}, s32[]{:S(2)}) async-start(s8[12582912]{0:T(1024)(128)(4,1)} %bitcast.234), calls=%async_computation.39 | async-start | bytes 8388608
  520.7 5.2 copy-start.16
  525.9 5.0 copy-start.5
  525.9 5.0 copy-start.14
  536.9 104.2 %reduce-scatter.35.cloned.1.call-start = ((), (), s32[]{:S(2)}) async-start(), calls=%async_computation.34 | async-start | bytes 1327104 | tf_op jit(solution)/shard_map/reduce_scatter | solution.py:42
  543.1 165.1 %reduce-scatter.33.cloned.1.call-start = ((), (), s32[]{:S(2)}) async-start(), calls=%async_computation.33 | async-start | bytes 1327104 | tf_op jit(solution)/shard_map/reduce_scatter | solution.py:42
  549.7 223.0 %reduce-scatter.31.cloned.1.call-start = ((), (), s32[]{:S(2)}) async-start(), calls=%async_computation.32 | async-start | bytes 442368 | tf_op jit(solution)/shard_map/reduce_scatter | solution.py:42
  549.9 5.8 copy-start.12
  549.9 5.8 copy-start.26
  557.2 281.9 %reduce-scatter.29.cloned.1.call-start = ((), (), s32[]{:S(2)}) async-start(), calls=%async_computation.31 | async-start | bytes 1105920 | tf_op jit(solution)/shard_map/reduce_scatter | solution.py:42
  560.4 7.4 copy-start.8
  568.9 145.5 %copy-start.28 = (bf16[3,64,1024]{2,1,0:T(8,128)(2,1)S(1)}, bf16[3,64,1024]{2,1,0:T(8,128)(2,1)}, u32[]{:S(2)}) copy-start(bf16[3,64,1024]{2,1,0:T(8,128)(2,1)} %copy-done.27) | copy-start | bytes 1179652
  568.9 145.5 %copy-start.30 = (bf16[3,64,1024]{2,1,0:T(8,128)(2,1)S(1)}, bf16[3,64,1024]{2,1,0:T(8,128)(2,1)}, u32[]{:S(2)}) copy-start(bf16[3,64,1024]{2,1,0:T(8,128)(2,1)} %copy-done.29) | copy-start | bytes 1179652
  571.8 268.9 %all-to-all-start.2 = ((bf16[256,2,768]{2,1,0:T(2,128)(2,1)}), bf16[256,2,768]{2,1,0:T(2,128)(2,1)S(1)}, u32[]{:S(2)}, u32[]{:S(2)}) async-start(bf16[256,2,768]{2,1,0:T(2,128)(2,1)} %copy.91), calls=%async_computation.10 | async-start | bytes 1572864 | tf_op jit(solution)/shard_map/all_to_all | solution.py:354
  714.4 127.1 %copy-start.57 = (s32[16]{0:T(128)S(1)}, s32[16]{0:T(128)}, u32[]{:S(2)}) copy-start(s32[16]{0:T(128)} %param.19) | copy-start | bytes 196
  714.4 128.4 %copy-start.1 = (bf16[32,16,768]{2,1,0:T(8,128)(2,1)S(1)}, bf16[32,16,768]{2,1,0:T(8,128)(2,1)}, u32[]{:S(2)}) copy-start(bf16[32,16,768]{2,1,0:T(8,128)(2,1)} %param.17) | copy-start | bytes 2359300
  (33 other events, 100.8 us)
Sparse Core Ops, SparseCore 0:
  39.1 18.6 all-gather.30
  59.9 19.6 all-gather.28
  123.8 27.3 reduce-scatter.12
  153.7 27.9 reduce-scatter.16
  340.0 19.6 all-gather.20
  361.1 19.6 all-gather.24
  462.5 19.6 all-gather.26
  483.7 19.6 all-gather.22
  509.4 27.9 reduce-scatter.26
  539.8 27.9 reduce-scatter.22
  571.2 69.7 reduce-scatter.34
  644.3 63.8 reduce-scatter.32
  711.5 61.2 reduce-scatter.30
  776.0 63.0 reduce-scatter.28
Sparse Core Ops, SparseCore 1:
  138.4 40.5 all-gather.14
  187.0 19.5 all-gather.18
  208.5 19.5 all-gather.12
  230.3 41.4 all-gather.16
  276.1 26.3 reduce-scatter.14
  305.0 27.9 reduce-scatter.18
  396.2 27.9 reduce-scatter.20
  426.6 27.9 reduce-scatter.24
where the time goes:
time: 859 us; the launch traced here: 850 us
  waiting for transfers between devices  452 us (53%)
  blocking collectives  153 us (18%)
  matrix products  136 us (16%)
  other arithmetic  55.4 us (6%)
  local copies, waits for them, and re-layouts  28.8 us (3%)
  between operations  16.9 us (2%)
    reduce_scatter x4, waiting for transfers between devices, scatter_weight(): lax.psum_scatter(grad.astype(jnp.bfloat16), 'dp', scatter_dimension=0, ti...  208 us
    reduce_scatter x8, waiting for transfers between devices, scatter_rows(): lax.psum_scatter(partial_sum.astype(jnp.bfloat16), 'tensor', scatter_dime...  131 us
    all_gather x8, waiting for transfers between devices, gather_rows(): return lax.all_gather(block, 'tensor', axis=0, tiled=True)  84.8 us
    unnamed x1, blocking collectives  40.2 us
    all_gather x1, blocking collectives, on_device(): project_full = lax.all_gather(project_weight, 'dp', axis=0, tiled=True)  32.5 us
    all_gather x1, blocking collectives, on_device(): lax.all_gather(attention_output_weight, 'dp', axis=0, tiled=True)  31.2 us
    all_to_all x1, blocking collectives, on_device(): lax.all_to_all(send_tokens, 'dp', split_axis=1, concat_axis=0, tiled=True)  27.4 us
    all_gather x1, waiting for transfers between devices, on_device(): down_full = lax.all_gather(feed_output_weight, 'dp', axis=0, tiled=True)  26.3 us
  transfers between devices with their start and end apart: 23, of which 16 were waited for; matrix products, arithmetic and copies ran while one was open for 18% of the time, Pallas kernels for 0%

commit v1 on v0

--- a/solution.py
+++ b/solution.py
@@ -3,10 +3,19 @@
 import jax.numpy as jnp
 from jax import lax
 from jax.sharding import PartitionSpec as P
+from jax.lax import all_gather
 
 HD = 64
 EPSILON = 1e-12
 MASKED = -1e30
+
+
+def blocks_create(load, base_x, mesh_name):
+    return jnp.split(
+        all_gather(jnp.concatenate([load, base_x], axis=1), mesh_name, tiled=True, axis=0),
+        [load.shape[1]],
+        axis=1,
+    )
 
 
 def norm_forward(value, gain, shift):
@@ -98,8 +107,7 @@
         inner_rows // piece_rows * n_tensor + owner_rows
     ) * piece_rows + inner_rows % piece_rows
     key_valid = position[None, :] < seq_length[:, None]
-    project_full = lax.all_gather(project_weight, "dp", axis=0, tiled=True)
-    output_full = lax.all_gather(attention_output_weight, "dp", axis=0, tiled=True)
+    project_full, output_full = blocks_create(project_weight, attention_output_weight, "dp")
     up_full = lax.all_gather(feed_input_weight, "dp", axis=0, tiled=True)
     down_full = lax.all_gather(feed_output_weight, "dp", axis=0, tiled=True)
     query_part = lax.dynamic_slice_in_dim(

time: 859 us -> 890 us (1.036)
  waiting for transfers between devices: 452 us -> 546 us
  blocking collectives: 153 us -> 93.7 us
    all_gather x2 -> x0, blocking collectives: 63.7 us -> none  [the longest x1 32.5 us: on_device(): project_full = lax.all_gather(project_weight, 'dp', axis=0, tiled=True)]
    all_gather x8, waiting for transfers between devices: 84.8 us -> 128 us  [gather_rows(): return lax.all_gather(block, 'tensor', axis=0, tiled=True)]
    all_gather x1, waiting for transfers between devices: 0.01 us -> 35.5 us  [on_device(): up_full = lax.all_gather(feed_input_weight, 'dp', axis=0, tiled=True)]
    all_gather x0 -> x1, waiting for transfers between devices: none -> 11.9 us  [blocks_create(): all_gather(jnp.concatenate([load, base_x], axis=1), mesh_name, tiled=True...]
  transfers between devices with their start and end apart: 23 -> 24, of which waited for: 16 -> 20; matrix products, arithmetic and copies ran while one was open for 18% -> 18% of each run, Pallas kernels for 0% -> 0%
where the time goes in v1:
time: 890 us; the launch traced here: 882 us
  waiting for transfers between devices  546 us (61%)
  matrix products  136 us (15%)
  blocking collectives  93.7 us (11%)
  other arithmetic  56 us (6%)
  local copies, waits for them, and re-layouts  27.4 us (3%)
  between operations  15.5 us (2%)
    reduce_scatter x4, waiting for transfers between devices, scatter_weight(): lax.psum_scatter(grad.astype(jnp.bfloat16), 'dp', scatter_dimension=0, ti...  208 us
    reduce_scatter x8, waiting for transfers between devices, scatter_rows(): lax.psum_scatter(partial_sum.astype(jnp.bfloat16), 'tensor', scatter_dime...  134 us
    all_gather x8, waiting for transfers between devices, gather_rows(): return lax.all_gather(block, 'tensor', axis=0, tiled=True)  128 us
    unnamed x1, blocking collectives  40.1 us
    all_gather x1, waiting for transfers between devices, on_device(): up_full = lax.all_gather(feed_input_weight, 'dp', axis=0, tiled=True)  35.5 us
    all_to_all x1, blocking collectives, on_device(): lax.all_to_all(send_tokens, 'dp', split_axis=1, concat_axis=0, tiled=True)  32 us
    all_gather x1, waiting for transfers between devices, on_device(): down_full = lax.all_gather(feed_output_weight, 'dp', axis=0, tiled=True)  26 us
    dot_general x2, matrix products, on_device(): jnp.dot(first_full[s], up_full, preferred_element_type=jnp.float32)  22.2 us
  transfers between devices with their start and end apart: 24, of which 20 were waited for; matrix products, arithmetic and copies ran while one was open for 18% of the time, Pallas kernels for 0%

profile of v1, /device:TPU:0, one launch (start us, length us, event | category | flops | bytes accessed | tf_op | source)
XLA Modules:
  0.0 881.9 jit_solution(17437990461061641188)
XLA Ops:
  10.5 32.0 %all_to_all.54 = bf16[32,16,768]{2,0,1:T(8,128)(2,1)S(1)} all-to-all(bf16[32,16,768]{2,0,1:T(8,128)(2,1)S(1)} %copy.78), channel_id=1, replica_groups=mesh['dp'=8,'tensor'=4] {'dp'}, dimensions={1} | all-to-all | bytes 1572864 | tf_op jit(solution)/shard_map/all_to_all | solution.py:98
  46.2 11.9 %all-gather.14.cloned.1.call-done = bf16[768,768]{1,0:T(8,128)(2,1)} async-done(((bf16[96,768]{1,0:T(8,128)(2,1)}), bf16[768,768]{1,0:T(8,128)(2,1)}) %all-gather.14.cloned.1.call-update) | async-done | bytes 1179664 | tf_op jit(solution)/shard_map/all_gather | solution.py:15
  58.0 20.5 %all-gather.34.cloned.1.call-done = bf16[1024,1,768]{2,0,1:T(8,128)(2,1)} async-done(((bf16[256,1,768]{2,0,1:T(8,128)(2,1)}), bf16[1024,1,768]{2,0,1:T(8,128)(2,1)}) %all-gather.34.cloned.1.call-update) | async-done | bytes 1572880 | tf_op jit(solution)/shard_map/all_gather | solution.py:41
  78.5 2.8 add_convert_fusion.4
  81.4 18.9 %all-gather.32.cloned.1.call-done = bf16[1024,1,768]{2,0,1:T(8,128)(2,1)} async-done(((bf16[256,1,768]{2,0,1:T(8,128)(2,1)}), bf16[1024,1,768]{2,0,1:T(8,128)(2,1)}) %all-gather.32.cloned.1.call-update) | async-done | bytes 1572880 | tf_op jit(solution)/shard_map/all_gather | solution.py:41
  100.3 2.5 add_convert_fusion.5
  103.0 2.3 fusion.125
  107.1 2.9 copy-done.2
  110.1 2.3 fusion.47
  112.4 2.0 convolution_convert_fusion.7
  115.0 2.3 fusion.126
  119.1 3.1 copy-done.3
  122.2 2.3 fusion.46
  127.2 15.5 %reduce-scatter.13.cloned.1.call-done = bf16[256,768]{1,0:T(8,128)(2,1)} async-done(((bf16[1024,768]{1,0:T(8,128)(2,1)}), bf16[256,768]{1,0:T(8,128)(2,1)}) %reduce-scatter.13.cloned.1.call-update) | async-done | bytes 393232 | tf_op jit(solution)/shard_map/reduce_scatter | solution.py:45
  143.9 29.1 %reduce-scatter.17.cloned.1.call-done = bf16[256,768]{1,0:T(8,128)(2,1)} async-done(((bf16[1024,768]{1,0:T(8,128)(2,1)}), bf16[256,768]{1,0:T(8,128)(2,1)}) %reduce-scatter.17.cloned.1.call-update) | async-done | bytes 393232 | tf_op jit(solution)/shard_map/reduce_scatter | solution.py:45
  175.9 2.3 fusion.68
  180.7 35.5 %all-gather.18.cloned.1.call-done = bf16[768,768]{1,0:T(8,128)(2,1)} async-done(((bf16[96,768]{1,0:T(8,128)(2,1)}), bf16[768,768]{1,0:T(8,128)(2,1)}) %all-gather.18.cloned.1.call-update) | async-done | bytes 1179664 | tf_op jit(solution)/shard_map/all_gather | solution.py:111
  216.3 20.5 %all-gather.22.cloned.1.call-done = bf16[1024,768]{1,0:T(8,128)(2,1)} async-done(((bf16[256,768]{1,0:T(8,128)(2,1)}), bf16[1024,768]{1,0:T(8,128)(2,1)}) %all-gather.22.cloned.1.call-update) | async-done | bytes 1572880 | tf_op jit(solution)/shard_map/all_gather | solution.py:41
  236.8 4.8 fusion.127
  241.6 17.0 %all-gather.16.cloned.1.call-done = bf16[1024,768]{1,0:T(8,128)(2,1)} async-done(((bf16[256,768]{1,0:T(8,128)(2,1)}), bf16[1024,768]{1,0:T(8,128)(2,1)}) %all-gather.16.cloned.1.call-update) | async-done | bytes 1572880 | tf_op jit(solution)/shard_map/all_gather | solution.py:41
  258.6 17.3 %multiply_convert_fusion.3 = (bf16[1024,768]{1,0:T(8,128)(2,1)}, f32[1024,768]{1,0:T(8,128)}, bf16[1024,768]{1,0:T(8,128)(2,1)}, f32[1024,768]{1,0:T(8,128)}, f32[1024,768]{1,0:T(8,128)}) fusion(f32[768]{0:T(1024)S(1)} %dynamic_slice.11, f32[1024,768]{1,0:T(8,128)} %fusion.127, bf16[1024,768]{1,0:T(8,128)(2,1)} %all-gather.16.cloned.1.call-done, ...), kind=kOutput, calls=%fused_computation.43 | convolution fusion | flops 1311768576 | bytes 18484224 | tf_op jit(solution)/shard_map/dot_general | solution.py:215
  275.9 26.0 %all-gather.20.cloned.1.call-done = bf16[768,768]{1,0:T(8,128)(2,1)} async-done(((bf16[96,768]{1,0:T(8,128)(2,1)}), bf16[768,768]{1,0:T(8,128)(2,1)}) %all-gather.20.cloned.1.call-update) | async-done | bytes 1179664 | tf_op jit(solution)/shard_map/all_gather | solution.py:112
  301.9 4.3 convolution_convert_fusion.6
  306.3 4.4 convolution_convert_fusion.4
  311.5 21.6 %all_to_all.55 = bf16[32,16,768]{2,0,1:T(8,128)(2,1)S(1)} all-to-all(bf16[32,16,768]{2,0,1:T(8,128)(2,1)S(1)} %copy.83), channel_id=1, replica_groups=mesh['dp'=8,'tensor'=4] {'dp'}, dimensions={1} | all-to-all | bytes 1572864 | tf_op jit(solution)/shard_map/all_to_all | solution.py:99
  333.3 30.5 %reduce-scatter.19.cloned.1.call-done = bf16[256,768]{1,0:T(8,128)(2,1)} async-done(((bf16[1024,768]{1,0:T(8,128)(2,1)}), bf16[256,768]{1,0:T(8,128)(2,1)}) %reduce-scatter.19.cloned.1.call-update) | async-done | bytes 393232 | tf_op jit(solution)/shard_map/reduce_scatter | solution.py:45
  367.5 3.2 fusion.116
  371.8 18.7 %all-gather.24.cloned.1.call-done = bf16[1024,768]{1,0:T(8,128)(2,1)} async-done(((bf16[256,768]{1,0:T(8,128)(2,1)}), bf16[1024,768]{1,0:T(8,128)(2,1)}) %all-gather.24.cloned.1.call-update) | async-done | bytes 1572880 | tf_op jit(solution)/shard_map/all_gather | solution.py:41
  390.5 4.8 fusion.128
  395.2 16.5 %all-gather.28.cloned.1.call-done = bf16[1024,768]{1,0:T(8,128)(2,1)} async-done(((bf16[256,768]{1,0:T(8,128)(2,1)}), bf16[1024,768]{1,0:T(8,128)(2,1)}) %all-gather.28.cloned.1.call-update) | async-done | bytes 1572880 | tf_op jit(solution)/shard_map/all_gather | solution.py:41
  411.7 11.5 %convert_reduce_fusion = (f32[768]{0:T(1024)}, bf16[1024,768]{1,0:T(8,128)(2,1)}, f32[768]{0:T(1024)}, bf16[1024,768]{1,0:T(8,128)(2,1)S(1)}) fusion(f32[1024,768]{1,0:T(8,128)} %get-tuple-element.152, f32[1024,768]{1,0:T(8,128)} %fusion.127, f32[768]{0:T(1024)} %copy-done.61, f32[1024,768]{1,0:T(8,128)} %fusion.128, f32[1024,768]{1,0:T(8,128)} %get-tuple-element.119, ...), kind=kOutput, calls=%fused_computation.26 | convolution fusion | flops 1234696704 | bytes 21636096 | tf_op jit(solution)/shard_map/dot_general | solution.py:240
  424.4 2.6 convolution_convert_fusion.3
  427.1 4.4 convolution_convert_fusion.2
  431.6 23.6 %reduce-scatter.21.cloned.1.call-done = bf16[256,768]{1,0:T(8,128)(2,1)} async-done(((bf16[1024,768]{1,0:T(8,128)(2,1)}), bf16[256,768]{1,0:T(8,128)(2,1)}) %reduce-scatter.21.cloned.1.call-update) | async-done | bytes 393232 | tf_op jit(solution)/shard_map/reduce_scatter | solution.py:45
  455.2 30.4 %reduce-scatter.25.cloned.1.call-done = bf16[256,768]{1,0:T(8,128)(2,1)} async-done(((bf16[1024,768]{1,0:T(8,128)(2,1)}), bf16[256,768]{1,0:T(8,128)(2,1)}) %reduce-scatter.25.cloned.1.call-update) | async-done | bytes 393232 | tf_op jit(solution)/shard_map/reduce_scatter | solution.py:45
  485.6 3.1 multiply_reduce_fusion.3
  488.8 2.9 fusion.115
  497.3 15.8 %all-gather.30.cloned.1.call-done = bf16[1024,768]{1,0:T(8,128)(2,1)} async-done(((bf16[256,768]{1,0:T(8,128)(2,1)}), bf16[1024,768]{1,0:T(8,128)(2,1)}) %all-gather.30.cloned.1.call-update) | async-done | bytes 1572880 | tf_op jit(solution)/shard_map/all_gather | solution.py:41
  513.2 2.3 convolution_convert_fusion.11
  515.5 6.1 multiply_reduce_fusion
  524.2 5.2 multiply_convert_fusion
  529.5 5.0 fusion.38
  535.8 2.0 fusion.42
  538.6 2.6 convolution_convert_fusion
  541.5 2.2 convolution_convert_fusion.12
  543.7 6.5 multiply_reduce_fusion.1
  552.8 5.2 multiply_convert_fusion.1
  558.0 5.0 fusion.36
  564.3 2.0 fusion.39
  566.4 2.6 convolution_convert_fusion.1
  569.1 3.5 fusion.131
  572.6 2.6 add_convert_fusion.2
  575.5 3.6 fusion.130
  579.1 2.5 add_convert_fusion.3
  584.5 2.1 fusion.129
  588.2 3.0 fusion.24
  591.3 2.4 add_convert_fusion.6
  595.6 4.4 reduce-scatter.23.cloned.1.call-done
  603.9 5.5 all-to-all-start.2
  610.3 62.9 %reduce-scatter.35.cloned.1.call-done = bf16[96,768]{1,0:T(8,128)(2,1)} async-done(((bf16[768,768]{1,0:T(8,128)(2,1)}), bf16[96,768]{1,0:T(8,128)(2,1)}) %reduce-scatter.35.cloned.1.call-update) | async-done | bytes 147472 | tf_op jit(solution)/shard_map/reduce_scatter | solution.py:51
  674.8 65.5 %reduce-scatter.33.cloned.1.call-done = bf16[96,768]{1,0:T(8,128)(2,1)} async-done(((bf16[768,768]{1,0:T(8,128)(2,1)}), bf16[96,768]{1,0:T(8,128)(2,1)}) %reduce-scatter.33.cloned.1.call-update) | async-done | bytes 147472 | tf_op jit(solution)/shard_map/reduce_scatter | solution.py:51
  748.6 40.1 %all-reduce.2 = (f32[32,48]{1,0:T(8,128)S(1)}, f32[32,240]{1,0:T(8,128)S(1)}) all-reduce(f32[32,48]{1,0:T(8,128)S(1)} %pad_maximum_fusion.5, f32[32,240]{1,0:T(8,128)} %concatenate.25), channel_id=13, replica_groups=mesh['dp'=8,'tensor'=4] {'dp','tensor'}, use_global_device_ids=true, to_apply=%region_34.35.clone | all-reduce | flops 9216 | bytes 73728
  790.5 14.3 %reduce-scatter.31.cloned.1.call-done = bf16[96,192]{1,0:T(8,128)(2,1)} async-done(((bf16[768,192]{1,0:T(8,128)(2,1)}), bf16[96,192]{1,0:T(8,128)(2,1)}) %reduce-scatter.31.cloned.1.call-update) | async-done | bytes 36880 | tf_op jit(solution)/shard_map/reduce_scatter | solution.py:51
  806.2 65.1 %reduce-scatter.29.cloned.1.call-done = bf16[96,576]{1,0:T(8,128)(2,1)} async-done(((bf16[768,576]{1,0:T(8,128)(2,1)}), bf16[96,576]{1,0:T(8,128)(2,1)}) %reduce-scatter.29.cloned.1.call-update) | async-done | bytes 110608 | tf_op jit(solution)/shard_map/reduce_scatter | solution.py:51
  (303 shorter events, 69.7 us)
Async XLA Ops:
  7.2 50.8 %all-gather.14.cloned.1.call-start = ((), (), s32[]{:S(2)}) async-start(), calls=%async_computation.15 | async-start | bytes 1327104 | tf_op jit(solution)/shard_map/all_gather | solution.py:15
  9.0 69.5 %all-gather.34.cloned.1.call-start = ((), (), s32[]{:S(2)}) async-start(), calls=%async_computation.37 | async-start | bytes 1966080 | tf_op jit(solution)/shard_map/all_gather | solution.py:41
  10.4 35.4 %copy-start.58 = (s32[16]{0:T(128)S(1)}, s32[16]{0:T(128)}, u32[]{:S(2)}) copy-start(s32[16]{0:T(128)} %param.19) | copy-start | bytes 196
  10.5 35.4 %copy-start.63 = (s32[16]{0:T(128)S(1)}, s32[16]{0:T(128)}, u32[]{:S(2)}) copy-start(s32[16]{0:T(128)} %param.18) | copy-start | bytes 196
  43.5 56.9 %all-gather.32.cloned.1.call-start = ((), (), s32[]{:S(2)}) async-start(), calls=%async_computation.36 | async-start | bytes 1966080 | tf_op jit(solution)/shard_map/all_gather | solution.py:41
  44.2 98.4 %reduce-scatter.13.cloned.1.call-start = ((), (), s32[]{:S(2)}) async-start(), calls=%async_computation.16 | async-start | bytes 1966080 | tf_op jit(solution)/shard_map/reduce_scatter | solution.py:45
  58.0 42.3 %copy-start.23 = (bf16[768,768]{1,0:T(8,128)(2,1)S(1)}, bf16[768,768]{1,0:T(8,128)(2,1)}, u32[]{:S(2)}) copy-start(bf16[768,768]{1,0:T(8,128)(2,1)} %all-gather.14.cloned.1.call-done) | copy-start | bytes 3538948
  81.4 33.6 %copy-start.17 = (bf16[1024,192]{0,1:T(8,128)(2,1)}, bf16[1024,192]{0,1:T(8,128)(2,1)S(1)}, u32[]{:S(2)}) copy-start(bf16[1024,192]{0,1:T(8,128)(2,1)S(1)} %get-tuple-element.127) | copy-start | bytes 1179652
  81.4 33.6 %copy-start.19 = (bf16[1024,192]{0,1:T(8,128)(2,1)}, bf16[1024,192]{0,1:T(8,128)(2,1)S(1)}, u32[]{:S(2)}) copy-start(bf16[1024,192]{0,1:T(8,128)(2,1)S(1)} %get-tuple-element.128) | copy-start | bytes 1179652
  107.1 5.3 copy-start.48
  112.4 4.9 copy-start.41
  114.5 58.6 %reduce-scatter.17.cloned.1.call-start = ((), (), s32[]{:S(2)}) async-start(), calls=%async_computation.21 | async-start | bytes 1966080 | tf_op jit(solution)/shard_map/reduce_scatter | solution.py:45
  117.4 4.8 copy-start.3
  117.4 4.8 copy-start.47
  119.1 5.4 copy-start.49
  124.5 50.1 %copy-start.29 = (bf16[3,64,1024]{2,1,0:T(8,128)(2,1)}, bf16[3,64,1024]{2,1,0:T(8,128)(2,1)S(1)}, u32[]{:S(2)}) copy-start(bf16[3,64,1024]{2,1,0:T(8,128)(2,1)S(1)} %fusion.46) | copy-start | bytes 1179652
  124.5 18.1 %copy-start.45 = (f32[768]{0:T(1024)S(1)}, f32[768]{0:T(1024)}, u32[]{:S(2)}) copy-start(f32[768]{0:T(1024)} %param.24) | copy-start | bytes 9220
  124.6 51.3 %copy-start.50 = (f32[768]{0:T(1024)S(1)}, f32[768]{0:T(1024)}, u32[]{:S(2)}) copy-start(f32[768]{0:T(1024)} %param.25) | copy-start | bytes 9220
  124.6 51.3 %copy-start.55 = (f32[768]{0:T(1024)S(1)}, f32[768]{0:T(1024)}, u32[]{:S(2)}) copy-start(f32[768]{0:T(1024)} %param.26) | copy-start | bytes 9220
  126.6 89.7 %all-gather.18.cloned.1.call-start = ((), (), s32[]{:S(2)}) async-start(), calls=%async_computation.18 | async-start | bytes 1327104 | tf_op jit(solution)/shard_map/all_gather | solution.py:111
  127.1 109.6 %all-gather.22.cloned.1.call-start = ((), (), s32[]{:S(2)}) async-start(), calls=%async_computation.22 | async-start | bytes 1966080 | tf_op jit(solution)/shard_map/all_gather | solution.py:41
  142.6 33.3 %copy-start.6 = (bf16[256,768]{1,0:T(8,128)(2,1)S(1)}, bf16[256,768]{1,0:T(8,128)(2,1)}, u32[]{:S(2)}) copy-start(bf16[256,768]{1,0:T(8,128)(2,1)} %reduce-scatter.13.cloned.1.call-done) | copy-start | bytes 1179652
  174.6 189.2 %copy-start.52 = (f32[256]{0:T(256)}, f32[256]{0:T(256)S(1)}, u32[]{:S(2)}) copy-start(f32[256]{0:T(256)S(1)} %get-tuple-element.164) | copy-start | bytes 3076
  175.9 187.9 %copy-start.51 = (f32[256]{0:T(256)}, f32[256]{0:T(256)S(1)}, u32[]{:S(2)}) copy-start(f32[256]{0:T(256)S(1)} %add_rsqrt_fusion.1) | copy-start | bytes 3076
  178.3 80.3 %all-gather.16.cloned.1.call-start = ((), (), s32[]{:S(2)}) async-start(), calls=%async_computation.17 | async-start | bytes 1966080 | tf_op jit(solution)/shard_map/all_gather | solution.py:41
  179.0 122.9 %all-gather.20.cloned.1.call-start = ((), (), s32[]{:S(2)}) async-start(), calls=%async_computation.19 | async-start | bytes 1327104 | tf_op jit(solution)/shard_map/all_gather | solution.py:112
  179.7 153.5 %reduce-scatter.15.cloned.1.call-start = ((), (), s32[]{:S(2)}) async-start(), calls=%async_computation.20 | async-start | bytes 1966080 | tf_op jit(solution)/shard_map/reduce_scatter | solution.py:45
  180.7 77.8 %copy-start.61 = (f32[768]{0:T(1024)}, f32[768]{0:T(1024)S(1)}, u32[]{:S(2)}) copy-start(f32[768]{0:T(1024)S(1)} %dynamic_slice.11) | copy-start | bytes 9220
  216.3 42.3 %copy-start.67 = (bf16[768,768]{1,0:T(8,128)(2,1)S(1)}, bf16[768,768]{1,0:T(8,128)(2,1)}, u32[]{:S(2)}) copy-start(bf16[768,768]{1,0:T(8,128)(2,1)} %all-gather.18.cloned.1.call-done) | copy-start | bytes 3538948
  306.2 57.5 %reduce-scatter.19.cloned.1.call-start = ((), (), s32[]{:S(2)}) async-start(), calls=%async_computation.23 | async-start | bytes 1966080 | tf_op jit(solution)/shard_map/reduce_scatter | solution.py:45
  310.7 53.1 %copy-start.7 = (bf16[256,768]{1,0:T(8,128)(2,1)S(1)}, bf16[256,768]{1,0:T(8,128)(2,1)}, u32[]{:S(2)}) copy-start(bf16[256,768]{1,0:T(8,128)(2,1)} %reduce-scatter.17.cloned.1.call-done) | copy-start | bytes 1179652
  310.7 53.1 %copy-start.56 = (f32[768]{0:T(1024)S(1)}, f32[768]{0:T(1024)}, u32[]{:S(2)}) copy-start(f32[768]{0:T(1024)} %param.26) | copy-start | bytes 9220
  310.7 53.1 %copy-start.62 = (f32[768]{0:T(1024)S(1)}, f32[768]{0:T(1024)}, u32[]{:S(2)}) copy-start(f32[768]{0:T(1024)} %param.30) | copy-start | bytes 9220
  310.7 79.7 %all-gather.24.cloned.1.call-start = ((), (), s32[]{:S(2)}) async-start(), calls=%async_computation.24 | async-start | bytes 1966080 | tf_op jit(solution)/shard_map/all_gather | solution.py:41
  333.2 33.0 %copy-start.57 = (f32[768]{0:T(1024)S(1)}, f32[768]{0:T(1024)}, u32[]{:S(2)}) copy-start(f32[768]{0:T(1024)} %param.31) | copy-start | bytes 9220
  370.7 41.0 %all-gather.28.cloned.1.call-start = ((), (), s32[]{:S(2)}) async-start(), calls=%async_computation.28 | async-start | bytes 1966080 | tf_op jit(solution)/shard_map/all_gather | solution.py:41
  371.6 83.6 %reduce-scatter.21.cloned.1.call-start = ((), (), s32[]{:S(2)}) async-start(), calls=%async_computation.25 | async-start | bytes 1966080 | tf_op jit(solution)/shard_map/reduce_scatter | solution.py:45
  411.7 12.7 %copy-start.68 = (bf16[768,768]{1,0:T(8,128)(2,1)S(1)}, bf16[768,768]{1,0:T(8,128)(2,1)}, u32[]{:S(2)}) copy-start(bf16[768,768]{1,0:T(8,128)(2,1)} %all-gather.18.cloned.1.call-done) | copy-start | bytes 3538948
  427.1 58.6 %reduce-scatter.25.cloned.1.call-start = ((), (), s32[]{:S(2)}) async-start(), calls=%async_computation.29 | async-start | bytes 1966080 | tf_op jit(solution)/shard_map/reduce_scatter | solution.py:45
  431.5 81.6 %all-gather.30.cloned.1.call-start = ((), (), s32[]{:S(2)}) async-start(), calls=%async_computation.30 | async-start | bytes 1966080 | tf_op jit(solution)/shard_map/all_gather | solution.py:41
  493.4 48.1 %all-gather.26.cloned.1.call-start = ((), (), s32[]{:S(2)}) async-start(), calls=%async_computation.26 | async-start | bytes 1966080 | tf_op jit(solution)/shard_map/all_gather | solution.py:41
  496.9 96.8 %reduce-scatter.27.cloned.1.call-start = ((), (), s32[]{:S(2)}) async-start(), calls=%async_computation.31 | async-start | bytes 1966080 | tf_op jit(solution)/shard_map/reduce_scatter | solution.py:45
  515.4 6.1 slice-start.3
  515.4 7.5 slice-start.4
  515.4 8.8 slice-start.5
  524.2 5.2 copy-start.20
  529.5 5.0 copy-start.4
  529.5 5.0 copy-start.18
  541.3 58.7 %reduce-scatter.23.cloned.1.call-start = ((), (), s32[]{:S(2)}) async-start(), calls=%async_computation.27 | async-start | bytes 1966080 | tf_op jit(solution)/shard_map/reduce_scatter | solution.py:45
  543.7 6.5 slice-start
  543.7 7.9 slice-start.1
  543.7 9.1 %slice-start.2 = ((s8[12582912]{0:T(1024)(128)(4,1)}), s8[4194304]{0:T(1024)(128)(4,1)S(1)}, s32[]{:S(2)}) async-start(s8[12582912]{0:T(1024)(128)(4,1)} %bitcast.226), calls=%async_computation.40 | async-start | bytes 8388608
  552.8 5.2 copy-start.16
  558.0 5.0 copy-start.5
  558.0 5.0 copy-start.14
  569.0 104.2 %reduce-scatter.35.cloned.1.call-start = ((), (), s32[]{:S(2)}) async-start(), calls=%async_computation.35 | async-start | bytes 1327104 | tf_op jit(solution)/shard_map/reduce_scatter | solution.py:51
  575.2 165.2 %reduce-scatter.33.cloned.1.call-start = ((), (), s32[]{:S(2)}) async-start(), calls=%async_computation.34 | async-start | bytes 1327104 | tf_op jit(solution)/shard_map/reduce_scatter | solution.py:51
  581.7 223.1 %reduce-scatter.31.cloned.1.call-start = ((), (), s32[]{:S(2)}) async-start(), calls=%async_computation.33 | async-start | bytes 442368 | tf_op jit(solution)/shard_map/reduce_scatter | solution.py:51
  588.1 283.3 %reduce-scatter.29.cloned.1.call-start = ((), (), s32[]{:S(2)}) async-start(), calls=%async_computation.32 | async-start | bytes 1105920 | tf_op jit(solution)/shard_map/reduce_scatter | solution.py:51
  591.3 8.7 copy-start.8
  601.1 145.5 %copy-start.36 = (bf16[3,64,1024]{2,1,0:T(8,128)(2,1)S(1)}, bf16[3,64,1024]{2,1,0:T(8,128)(2,1)}, u32[]{:S(2)}) copy-start(bf16[3,64,1024]{2,1,0:T(8,128)(2,1)} %copy-done.35) | copy-start | bytes 1179652
  603.9 269.1 %all-to-all-start.2 = ((bf16[256,2,768]{2,1,0:T(2,128)(2,1)}), bf16[256,2,768]{2,1,0:T(2,128)(2,1)S(1)}, u32[]{:S(2)}, u32[]{:S(2)}) async-start(bf16[256,2,768]{2,1,0:T(2,128)(2,1)} %copy.91), calls=%async_computation.10 | async-start | bytes 1572864 | tf_op jit(solution)/shard_map/all_to_all | solution.py:362
  746.5 127.3 %copy-start.60 = (s32[16]{0:T(128)S(1)}, s32[16]{0:T(128)}, u32[]{:S(2)}) copy-start(s32[16]{0:T(128)} %param.19) | copy-start | bytes 196
  746.5 128.6 %copy-start.1 = (bf16[32,16,768]{2,1,0:T(8,128)(2,1)S(1)}, bf16[32,16,768]{2,1,0:T(8,128)(2,1)}, u32[]{:S(2)}) copy-start(bf16[32,16,768]{2,1,0:T(8,128)(2,1)} %param.17) | copy-start | bytes 2359300
  (38 other events, 119.5 us)
Sparse Core Ops, SparseCore 0:
  10.8 47.2 all-gather.13
  60.2 18.3 all-gather.33
  80.7 19.6 all-gather.31
  114.6 28.0 reduce-scatter.12
  145.0 28.0 reduce-scatter.16
  175.1 41.1 all-gather.17
  218.4 18.3 all-gather.21
  238.9 19.6 all-gather.15
  260.7 41.1 all-gather.19
  306.4 26.7 reduce-scatter.14
  335.7 28.0 reduce-scatter.18
  370.8 19.6 all-gather.23
  392.0 19.6 all-gather.27
  427.2 27.9 reduce-scatter.20
  457.6 27.9 reduce-scatter.24
  493.5 19.6 all-gather.29
  514.6 19.6 all-gather.25
  541.4 28.0 reduce-scatter.26
  572.0 27.9 reduce-scatter.22
  603.2 69.8 reduce-scatter.34
  676.6 63.7 reduce-scatter.32
  743.6 61.1 reduce-scatter.30
  808.2 63.1 reduce-scatter.28
